TPU v7x, 32 devices: a whole 2x2x4 slice. The times are simulated.
32 devices in a mesh: section: 4 (over z), rep: 8 (over y, x, core).
Axes of the slice: x: 2, y: 2, z: 4, core: 2. Of those that a mesh axis runs over, the one named last changes fastest.
Arguments:
- tokens: bfloat16 [4, 1024, 1024], P(None, 'rep'), may hold values from -6 to 6
- replica_of_row: int32 [4, 1024, 1], P(None, 'rep'), may hold values from 0 to 15; in each aligned block of 128 rows (0 to 127, 128 to 255, ..., all dimensions but the last counted through in order) at most 12 rows name the same one
- widths: int32 [16], replicated, may hold values from 512 to 1024, as said below
- placement: int32 [16], replicated, may hold values from 0 to 23, as said below
- gains: float32 [4, 24, 1024], P('section', 'rep'), may hold values from 0.5 to 1.5
- weights: bfloat16 [4, 24, 1024, 1024], P('section', 'rep'), may hold values from -0.1875 to 0.1875
Outputs:
- final: bfloat16 [4, 1024, 1024], P(None, 'rep', 'section')
Inputs may be any that keep to these rules, and one draw needn't show every extreme that they name: `widths`: multiples of 128 from 512 to 1024. `placement`: distinct slots; slot g lies on index g // 3 of rep. `replica_of_row`: within the 128 tokens of one index of rep in one micro-batch, no replica is named by more than 12 tokens.
All inputs are finite; a program needn't handle non-finite values.
Results may differ from a plain program's by a relative error of at most 0.008.
Values may be sent and summed in bfloat16 or wider, within the bound.
No kernel may reach another device: no remote copies, remote signals or barrier semaphores. Data moves between devices by JAX's collectives and lax.ppermute only.
A program may use at most 64 MiB of HBM per device.

v0:
```python
import jax
import jax.numpy as jnp
from jax import lax
from jax.sharding import PartitionSpec as P

epsilon = 1e-05


def shifted(x, axis, by):
    length = lax.axis_size(axis)
    pairs = [(i, i + by) for i in range(length) if 0 <= i + by < length]
    return lax.ppermute(x, axis, pairs)


def on_device(tokens, replica_of_row, widths, placement, gains, weights):
    batches, row_count, width_max = tokens.shape
    rep_count = lax.axis_size("rep")
    section_count = lax.axis_size("section")
    slot_count = weights.shape[1]
    replica_count = widths.shape[0]
    total_slots = slot_count * rep_count
    capacity = (3 * row_count + 2 * replica_count - 1) // (2 * replica_count)
    section_id = lax.axis_index("section")
    rep_id = lax.axis_index("rep")
    final_section = section_count - 1
    features = jnp.arange(width_max, dtype=jnp.int32)
    replica_ids = jnp.arange(replica_count, dtype=jnp.int32)
    global_ids = rep_id * slot_count + jnp.arange(slot_count, dtype=jnp.int32)
    slot_width = jnp.sum(
        (placement[None, :] == global_ids[:, None]).astype(jnp.int32) * widths[None, :], axis=1
    )
    slot_live = (features[None, :] < slot_width[:, None]).astype(jnp.float32)
    slot_scale = 1.0 / jnp.maximum(slot_width, 1).astype(jnp.float32)
    section_gain = gains[0]
    section_weight = weights[0]
    slot_targets = jnp.arange(total_slots * capacity, dtype=jnp.int32)
    slot_numbers = jnp.arange(total_slots, dtype=jnp.int32)

    def routing(row_replica):
        picked = (row_replica[:, None] == replica_ids[None, :]).astype(jnp.int32)
        slot_of_row = jnp.sum(picked * placement[None, :], axis=1)
        row_width = jnp.sum(picked * widths[None, :], axis=1)
        slot_hits = (slot_of_row[:, None] == slot_numbers[None, :]).astype(jnp.int32)
        earlier = jnp.cumsum(slot_hits, axis=0) - slot_hits
        position = jnp.sum(earlier * slot_hits, axis=1)
        target = slot_of_row * capacity + position
        routing_table = (slot_targets[:, None] == target[None, :]).astype(jnp.bfloat16)
        return (routing_table, row_width)

    def update(buffer):
        float_rows = buffer.astype(jnp.float32)
        mean_square = jnp.sum(float_rows * float_rows, axis=-1) * slot_scale[None, :, None]
        lowered = (
            float_rows
            * lax.rsqrt(mean_square + epsilon)[..., None]
            * section_gain[None, :, None, :]
        ).astype(jnp.bfloat16)
        projected = jnp.einsum(
            "nscd,sde->nsce", lowered, section_weight, preferred_element_type=jnp.float32
        )
        return (float_rows + jax.nn.silu(projected) * slot_live[None, :, None, :]).astype(
            jnp.bfloat16
        )

    def unchanged(buffer):
        return buffer

    tick_count = batches + section_count - 1
    routing_tables, row_widths = jax.vmap(routing)(replica_of_row[:, :, 0])
    entering = jnp.where(
        features[None, None, :] < row_widths[:, :, None], tokens, jnp.zeros((), jnp.bfloat16)
    )
    outgoing = jnp.einsum(
        "mgr,mrd->mgd", routing_tables, entering, preferred_element_type=jnp.float32
    ).astype(jnp.bfloat16)
    outgoing = outgoing.reshape(batches, rep_count, slot_count * capacity, width_max)
    arrived_all = lax.all_to_all(outgoing, "rep", split_axis=1, concat_axis=1, tiled=True)
    arrived_all = arrived_all.reshape(batches, rep_count, slot_count, capacity, width_max)

    def tick(counter, carry):
        incoming, outbuf = carry
        index = counter - section_id
        valid = (index >= 0) & (index < batches)
        clipped = jnp.clip(index, 0, batches - 1)
        first_input = lax.dynamic_index_in_dim(arrived_all, clipped, 0, keepdims=False)
        current = jnp.where(section_id == 0, first_input, incoming)
        updated = lax.cond(valid, update, unchanged, current)
        storing = valid & (section_id == final_section)
        stored = lax.dynamic_update_index_in_dim(outbuf, updated, clipped, 0)
        outbuf = jnp.where(storing, stored, outbuf)
        incoming = shifted(updated, "section", 1)
        return (incoming, outbuf)

    start_slots = jnp.zeros((rep_count, slot_count, capacity, width_max), jnp.bfloat16)
    start_out = jnp.zeros((batches, rep_count, slot_count, capacity, width_max), jnp.bfloat16)
    last_slots, slot_results = lax.fori_loop(0, tick_count, tick, (start_slots, start_out))
    returned = lax.all_to_all(
        slot_results.reshape(batches, rep_count, slot_count * capacity, width_max),
        "rep",
        split_axis=1,
        concat_axis=1,
        tiled=True,
    )
    flat_back = returned.reshape(batches, total_slots * capacity, width_max)
    final_rows = jnp.einsum(
        "mgr,mgd->mrd", routing_tables, flat_back, preferred_element_type=jnp.float32
    ).astype(jnp.bfloat16)
    contribution = jnp.where(
        section_id == final_section, final_rows.astype(jnp.float32), jnp.zeros((), jnp.float32)
    )
    gathered = lax.psum_scatter(
        contribution.astype(jnp.bfloat16), "section", scatter_dimension=2, tiled=True
    )
    return gathered


def solution(mesh):
    placed = (
        P(None, "rep", None),
        P(None, "rep", None),
        P(),
        P(),
        P("section", "rep", None),
        P("section", "rep", None, None),
    )
    return jax.shard_map(
        on_device, mesh=mesh, in_specs=placed, out_specs=P(None, "rep", "section"), check_vma=False
    )
```

profile of v0, /device:TPU:0, one launch (start us, length us, event | category | flops | bytes accessed | tf_op | source)
XLA Modules:
  0.0 275.3 jit_solution(11272264600902718)
XLA Ops:
  8.0 2.1 convolution_convert_fusion
  10.1 3.2 %copy.37 = bf16[4,288,1024]{2,0,1:T(4,128)(2,1)} copy(bf16[4,288,1024]{2,1,0:T(8,128)(2,1)S(1)} %convolution_convert_fusion) | data formatting | bytes 4718592 | tf_op jit(solution)/shard_map/convert_element_type | solution.py:75
  13.3 5.3 %all-to-all-start = ((bf16[4,8,36,1024]{3,0,2,1:T(4,128)(2,1)}), bf16[4,8,36,1024]{3,0,2,1:T(4,128)(2,1)S(1)}, u32[]{:S(2)}, u32[]{:S(2)}) async-start(bf16[4,8,36,1024]{3,0,2,1:T(4,128)(2,1)} %bitcast.37), calls=%async_computation | async-start | bytes 4718592 | tf_op jit(solution)/shard_map/all_to_all | solution.py:77
  19.0 29.1 %all-to-all-done = bf16[4,8,36,1024]{3,0,2,1:T(4,128)(2,1)S(1)} async-done(((bf16[4,8,36,1024]{3,0,2,1:T(4,128)(2,1)}), bf16[4,8,36,1024]{3,0,2,1:T(4,128)(2,1)S(1)}, u32[]{:S(2)}, u32[]{:S(2)}) %all-to-all-start) | async-done | bytes 2359328 | tf_op jit(solution)/shard_map/all_to_all | solution.py:77
  48.1 2.7 copy.38
  50.9 1.7 broadcast_in_dim.47.clone
  52.6 129.7 %while.17 = (s32[]{:T(128)}, bf16[8,3,12,1024]{3,0,2,1:T(8,128)(2,1)S(1)}, bf16[4,8,3,12,1024]{4,1,3,2,0:T(8,128)(2,1)}, s32[]{:T(128)}, pred[]{:T(512)}, /*inde...) while((s32[]{:T(128)}, ...), condition=%wide.region_9.10_spmd.clone, body=%wide.region_5.9_spmd.clone.sunk | while | flops 608999680 | bytes 19899208 | solution.py:96
  54.6 4.7 %conditional.3 = (bf16[8,3,12,1024]{3,2,0,1:T(8,128)(2,1)S(1)}) conditional(s32[]{:T(128)} %convert_element_type.86, bf16[8,3,12,1024]{3,2,0,1:T(8,128)(2,1)S(1)} %bitcast_select_fusion.2, (bf16[8,3,12,1024]{3,2,0,1:T(8,128)(2,1)S(1)}, f32[3]{0:T(128)S(1)}, f32[1,3,1024]{2,1,0:T(4,128)S(1)}, bf16[3,1024,1024]{2,1,0:T(8,128)(2,1)}, ...), branch_computations={%region_6.6_spmd, %region_7.8_spmd} | conditional | flops 608403712 | bytes 9269780 | solution.py:87
  55.0 4.3 %fusion.7 = bf16[8,3,12,1024]{3,2,0,1:T(8,128)(2,1)S(1)} fusion(bf16[8,3,12,1024]{3,2,0,1:T(8,128)(2,1)S(1)} %copy.80, bf16[3,1024,1024]{2,1,0:T(8,128)(2,1)} %get-tuple-element.218, f32[3,1024]{1,0:T(4,128)S(1)} %get-tuple-element.219, f32[3,1024]{1,0:T(4,128)S(1)} %bitcast.39, f32[8,3,12]{2,0,1:T(8,128)S(1)} %add_rsqrt_fusion), kind=kOutput, calls=%fused_computation.9 | convolution fusion | flops 607518720 | bytes 7496832 | tf_op jit(solution)/shard_map/while/body/eval_jaxpr/cond/branch_1_fun/nscd,sde->nsce/dot_general | solution.py:58
  62.6 8.5 %collective-permute-done = bf16[8,3,12,1024]{3,0,2,1:T(8,128)(2,1)S(1)} collective-permute-done((bf16[8,3,12,1024]{3,0,2,1:T(8,128)(2,1)S(1)}, bf16[8,3,12,1024]{3,0,2,1:T(8,128)(2,1)S(1)}, u32[]{:S(2)}, u32[]{:S(2)}) %collective-permute-start) | collective-permute-done | bytes 589856 | tf_op jit(solution)/shard_map/while/body/eval_jaxpr/ppermute | solution.py:12
  73.1 4.7 %conditional.3 = (bf16[8,3,12,1024]{3,2,0,1:T(8,128)(2,1)S(1)}) conditional(s32[]{:T(128)} %convert_element_type.86, bf16[8,3,12,1024]{3,2,0,1:T(8,128)(2,1)S(1)} %bitcast_select_fusion.2, (bf16[8,3,12,1024]{3,2,0,1:T(8,128)(2,1)S(1)}, f32[3]{0:T(128)S(1)}, f32[1,3,1024]{2,1,0:T(4,128)S(1)}, bf16[3,1024,1024]{2,1,0:T(8,128)(2,1)}, ...), branch_computations={%region_6.6_spmd, %region_7.8_spmd} | conditional | flops 608403712 | bytes 9269780 | solution.py:87
  73.5 4.3 %fusion.7 = bf16[8,3,12,1024]{3,2,0,1:T(8,128)(2,1)S(1)} fusion(bf16[8,3,12,1024]{3,2,0,1:T(8,128)(2,1)S(1)} %copy.80, bf16[3,1024,1024]{2,1,0:T(8,128)(2,1)} %get-tuple-element.218, f32[3,1024]{1,0:T(4,128)S(1)} %get-tuple-element.219, f32[3,1024]{1,0:T(4,128)S(1)} %bitcast.39, f32[8,3,12]{2,0,1:T(8,128)S(1)} %add_rsqrt_fusion), kind=kOutput, calls=%fused_computation.9 | convolution fusion | flops 607518720 | bytes 7496832 | tf_op jit(solution)/shard_map/while/body/eval_jaxpr/cond/branch_1_fun/nscd,sde->nsce/dot_general | solution.py:58
  78.2 4.4 %collective-permute-start = (bf16[8,3,12,1024]{3,0,2,1:T(8,128)(2,1)S(1)}, bf16[8,3,12,1024]{3,0,2,1:T(8,128)(2,1)S(1)}, u32[]{:S(2)}, u32[]{:S(2)}) collective-permute-start(bf16[8,3,12,1024]{3,0,2,1:T(8,128)(2,1)S(1)} %copy.66), channel_id=1, source_target_pairs={{0,8},{8,16},{16,24},{1,9},{9,17},{17,25},{2,10},{10,18},{18,26},{... | collective-permute-start | bytes 1769480 | tf_op jit(solution)/shard_map/while/body/eval_jaxpr/ppermute | solution.py:12
  84.2 7.7 %collective-permute-done = bf16[8,3,12,1024]{3,0,2,1:T(8,128)(2,1)S(1)} collective-permute-done((bf16[8,3,12,1024]{3,0,2,1:T(8,128)(2,1)S(1)}, bf16[8,3,12,1024]{3,0,2,1:T(8,128)(2,1)S(1)}, u32[]{:S(2)}, u32[]{:S(2)}) %collective-permute-start) | collective-permute-done | bytes 589856 | tf_op jit(solution)/shard_map/while/body/eval_jaxpr/ppermute | solution.py:12
  93.9 4.7 %conditional.3 = (bf16[8,3,12,1024]{3,2,0,1:T(8,128)(2,1)S(1)}) conditional(s32[]{:T(128)} %convert_element_type.86, bf16[8,3,12,1024]{3,2,0,1:T(8,128)(2,1)S(1)} %bitcast_select_fusion.2, (bf16[8,3,12,1024]{3,2,0,1:T(8,128)(2,1)S(1)}, f32[3]{0:T(128)S(1)}, f32[1,3,1024]{2,1,0:T(4,128)S(1)}, bf16[3,1024,1024]{2,1,0:T(8,128)(2,1)}, ...), branch_computations={%region_6.6_spmd, %region_7.8_spmd} | conditional | flops 608403712 | bytes 9269780 | solution.py:87
  94.3 4.3 %fusion.7 = bf16[8,3,12,1024]{3,2,0,1:T(8,128)(2,1)S(1)} fusion(bf16[8,3,12,1024]{3,2,0,1:T(8,128)(2,1)S(1)} %copy.80, bf16[3,1024,1024]{2,1,0:T(8,128)(2,1)} %get-tuple-element.218, f32[3,1024]{1,0:T(4,128)S(1)} %get-tuple-element.219, f32[3,1024]{1,0:T(4,128)S(1)} %bitcast.39, f32[8,3,12]{2,0,1:T(8,128)S(1)} %add_rsqrt_fusion), kind=kOutput, calls=%fused_computation.9 | convolution fusion | flops 607518720 | bytes 7496832 | tf_op jit(solution)/shard_map/while/body/eval_jaxpr/cond/branch_1_fun/nscd,sde->nsce/dot_general | solution.py:58
  99.0 4.4 %collective-permute-start = (bf16[8,3,12,1024]{3,0,2,1:T(8,128)(2,1)S(1)}, bf16[8,3,12,1024]{3,0,2,1:T(8,128)(2,1)S(1)}, u32[]{:S(2)}, u32[]{:S(2)}) collective-permute-start(bf16[8,3,12,1024]{3,0,2,1:T(8,128)(2,1)S(1)} %copy.66), channel_id=1, source_target_pairs={{0,8},{8,16},{16,24},{1,9},{9,17},{17,25},{2,10},{10,18},{18,26},{... | collective-permute-start | bytes 1769480 | tf_op jit(solution)/shard_map/while/body/eval_jaxpr/ppermute | solution.py:12
  104.9 6.8 %collective-permute-done = bf16[8,3,12,1024]{3,0,2,1:T(8,128)(2,1)S(1)} collective-permute-done((bf16[8,3,12,1024]{3,0,2,1:T(8,128)(2,1)S(1)}, bf16[8,3,12,1024]{3,0,2,1:T(8,128)(2,1)S(1)}, u32[]{:S(2)}, u32[]{:S(2)}) %collective-permute-start) | collective-permute-done | bytes 589856 | tf_op jit(solution)/shard_map/while/body/eval_jaxpr/ppermute | solution.py:12
  113.8 4.7 %conditional.3 = (bf16[8,3,12,1024]{3,2,0,1:T(8,128)(2,1)S(1)}) conditional(s32[]{:T(128)} %convert_element_type.86, bf16[8,3,12,1024]{3,2,0,1:T(8,128)(2,1)S(1)} %bitcast_select_fusion.2, (bf16[8,3,12,1024]{3,2,0,1:T(8,128)(2,1)S(1)}, f32[3]{0:T(128)S(1)}, f32[1,3,1024]{2,1,0:T(4,128)S(1)}, bf16[3,1024,1024]{2,1,0:T(8,128)(2,1)}, ...), branch_computations={%region_6.6_spmd, %region_7.8_spmd} | conditional | flops 608403712 | bytes 9269780 | solution.py:87
  114.2 4.3 %fusion.7 = bf16[8,3,12,1024]{3,2,0,1:T(8,128)(2,1)S(1)} fusion(bf16[8,3,12,1024]{3,2,0,1:T(8,128)(2,1)S(1)} %copy.80, bf16[3,1024,1024]{2,1,0:T(8,128)(2,1)} %get-tuple-element.218, f32[3,1024]{1,0:T(4,128)S(1)} %get-tuple-element.219, f32[3,1024]{1,0:T(4,128)S(1)} %bitcast.39, f32[8,3,12]{2,0,1:T(8,128)S(1)} %add_rsqrt_fusion), kind=kOutput, calls=%fused_computation.9 | convolution fusion | flops 607518720 | bytes 7496832 | tf_op jit(solution)/shard_map/while/body/eval_jaxpr/cond/branch_1_fun/nscd,sde->nsce/dot_general | solution.py:58
  118.9 4.4 %collective-permute-start = (bf16[8,3,12,1024]{3,0,2,1:T(8,128)(2,1)S(1)}, bf16[8,3,12,1024]{3,0,2,1:T(8,128)(2,1)S(1)}, u32[]{:S(2)}, u32[]{:S(2)}) collective-permute-start(bf16[8,3,12,1024]{3,0,2,1:T(8,128)(2,1)S(1)} %copy.66), channel_id=1, source_target_pairs={{0,8},{8,16},{16,24},{1,9},{9,17},{17,25},{2,10},{10,18},{18,26},{... | collective-permute-start | bytes 1769480 | tf_op jit(solution)/shard_map/while/body/eval_jaxpr/ppermute | solution.py:12
  124.8 6.0 %collective-permute-done = bf16[8,3,12,1024]{3,0,2,1:T(8,128)(2,1)S(1)} collective-permute-done((bf16[8,3,12,1024]{3,0,2,1:T(8,128)(2,1)S(1)}, bf16[8,3,12,1024]{3,0,2,1:T(8,128)(2,1)S(1)}, u32[]{:S(2)}, u32[]{:S(2)}) %collective-permute-start) | collective-permute-done | bytes 589856 | tf_op jit(solution)/shard_map/while/body/eval_jaxpr/ppermute | solution.py:12
  133.2 9.1 %collective-permute-start = (bf16[8,3,12,1024]{3,0,2,1:T(8,128)(2,1)S(1)}, bf16[8,3,12,1024]{3,0,2,1:T(8,128)(2,1)S(1)}, u32[]{:S(2)}, u32[]{:S(2)}) collective-permute-start(bf16[8,3,12,1024]{3,0,2,1:T(8,128)(2,1)S(1)} %copy.66), channel_id=1, source_target_pairs={{0,8},{8,16},{16,24},{1,9},{9,17},{17,25},{2,10},{10,18},{18,26},{... | collective-permute-start | bytes 1769480 | tf_op jit(solution)/shard_map/while/body/eval_jaxpr/ppermute | solution.py:12
  143.9 6.1 %collective-permute-done = bf16[8,3,12,1024]{3,0,2,1:T(8,128)(2,1)S(1)} collective-permute-done((bf16[8,3,12,1024]{3,0,2,1:T(8,128)(2,1)S(1)}, bf16[8,3,12,1024]{3,0,2,1:T(8,128)(2,1)S(1)}, u32[]{:S(2)}, u32[]{:S(2)}) %collective-permute-start) | collective-permute-done | bytes 589856 | tf_op jit(solution)/shard_map/while/body/eval_jaxpr/ppermute | solution.py:12
  152.4 4.4 %collective-permute-start = (bf16[8,3,12,1024]{3,0,2,1:T(8,128)(2,1)S(1)}, bf16[8,3,12,1024]{3,0,2,1:T(8,128)(2,1)S(1)}, u32[]{:S(2)}, u32[]{:S(2)}) collective-permute-start(bf16[8,3,12,1024]{3,0,2,1:T(8,128)(2,1)S(1)} %copy.66), channel_id=1, source_target_pairs={{0,8},{8,16},{16,24},{1,9},{9,17},{17,25},{2,10},{10,18},{18,26},{... | collective-permute-start | bytes 1769480 | tf_op jit(solution)/shard_map/while/body/eval_jaxpr/ppermute | solution.py:12
  158.4 5.8 %collective-permute-done = bf16[8,3,12,1024]{3,0,2,1:T(8,128)(2,1)S(1)} collective-permute-done((bf16[8,3,12,1024]{3,0,2,1:T(8,128)(2,1)S(1)}, bf16[8,3,12,1024]{3,0,2,1:T(8,128)(2,1)S(1)}, u32[]{:S(2)}, u32[]{:S(2)}) %collective-permute-start) | collective-permute-done | bytes 589856 | tf_op jit(solution)/shard_map/while/body/eval_jaxpr/ppermute | solution.py:12
  166.6 8.4 %collective-permute-start = (bf16[8,3,12,1024]{3,0,2,1:T(8,128)(2,1)S(1)}, bf16[8,3,12,1024]{3,0,2,1:T(8,128)(2,1)S(1)}, u32[]{:S(2)}, u32[]{:S(2)}) collective-permute-start(bf16[8,3,12,1024]{3,0,2,1:T(8,128)(2,1)S(1)} %copy.66), channel_id=1, source_target_pairs={{0,8},{8,16},{16,24},{1,9},{9,17},{17,25},{2,10},{10,18},{18,26},{... | collective-permute-start | bytes 1769480 | tf_op jit(solution)/shard_map/while/body/eval_jaxpr/ppermute | solution.py:12
  176.5 5.8 %collective-permute-done = bf16[8,3,12,1024]{3,0,2,1:T(8,128)(2,1)S(1)} collective-permute-done((bf16[8,3,12,1024]{3,0,2,1:T(8,128)(2,1)S(1)}, bf16[8,3,12,1024]{3,0,2,1:T(8,128)(2,1)S(1)}, u32[]{:S(2)}, u32[]{:S(2)}) %collective-permute-start) | collective-permute-done | bytes 589856 | tf_op jit(solution)/shard_map/while/body/eval_jaxpr/ppermute | solution.py:12
  182.3 3.5 %copy.41 = bf16[4,8,36,1024]{3,0,2,1:T(4,128)(2,1)S(1)} copy(bf16[4,8,36,1024]{3,1,2,0:T(8,128)(2,1)} %bitcast.8) | data formatting | bytes 4718592 | tf_op jit(solution)/shard_map/reshape | solution.py:98
  185.8 46.8 %all_to_all.10 = bf16[4,8,36,1024]{3,0,2,1:T(4,128)(2,1)S(1)} all-to-all(bf16[4,8,36,1024]{3,0,2,1:T(4,128)(2,1)S(1)} %copy.41), channel_id=1, replica_groups=mesh['section'=4,'rep'=8] {'rep'}, dimensions={1} | all-to-all | bytes 4718592 | tf_op jit(solution)/shard_map/all_to_all | solution.py:97
  232.6 2.6 select_convert_fusion
  235.3 33.2 %reduce-scatter.2.cloned.1.call-done = bf16[4,128,256]{2,1,0:T(8,128)(2,1)} async-done(((bf16[4,128,1024]{2,1,0:T(8,128)(2,1)}), bf16[4,128,256]{2,1,0:T(8,128)(2,1)}) %reduce-scatter.2.cloned.1.call-update) | async-done | bytes 262160 | tf_op jit(solution)/shard_map/reduce_scatter | solution.py:111
  (76 shorter events, 31.8 us)
Async XLA Ops:
  13.3 5.4 %copy-start = (f32[1,3,1024]{2,0,1:T(1,128)S(1)}, f32[1,3,1024]{2,0,1:T(1,128)}, u32[]{:S(2)}) copy-start(f32[1,3,1024]{2,0,1:T(1,128)} %param.14) | copy-start | bytes 36868
  13.3 5.4 %copy-start.1 = (s32[16]{0:T(128)S(1)}, s32[16]{0:T(128)}, u32[]{:S(2)}) copy-start(s32[16]{0:T(128)} %param.13) | copy-start | bytes 196
  13.3 5.4 %copy-start.2 = (s32[16]{0:T(128)S(1)}, s32[16]{0:T(128)}, u32[]{:S(2)}) copy-start(s32[16]{0:T(128)} %param.12) | copy-start | bytes 196
  13.3 34.8 %all-to-all-start = ((bf16[4,8,36,1024]{3,0,2,1:T(4,128)(2,1)}), bf16[4,8,36,1024]{3,0,2,1:T(4,128)(2,1)S(1)}, u32[]{:S(2)}, u32[]{:S(2)}) async-start(bf16[4,8,36,1024]{3,0,2,1:T(4,128)(2,1)} %bitcast.37), calls=%async_computation | async-start | bytes 4718592 | tf_op jit(solution)/shard_map/all_to_all | solution.py:77
  18.7 249.7 %reduce-scatter.2.cloned.1.call-start = ((), (), s32[]{:S(2)}) async-start(), calls=%async_computation.3 | async-start | bytes 1310720 | tf_op jit(solution)/shard_map/reduce_scatter | solution.py:111
  59.7 11.4 %collective-permute-start = (bf16[8,3,12,1024]{3,0,2,1:T(8,128)(2,1)S(1)}, bf16[8,3,12,1024]{3,0,2,1:T(8,128)(2,1)S(1)}, u32[]{:S(2)}, u32[]{:S(2)}) collective-permute-start(bf16[8,3,12,1024]{3,0,2,1:T(8,128)(2,1)S(1)} %copy.66), channel_id=1, source_target_pairs={{0,8},{8,16},{16,24},{1,9},{9,17},{17,25},{2,10},{10,18},{18,26},{... | collective-permute-start | bytes 1769480 | tf_op jit(solution)/shard_map/while/body/eval_jaxpr/ppermute | solution.py:12
  78.2 13.6 %collective-permute-start = (bf16[8,3,12,1024]{3,0,2,1:T(8,128)(2,1)S(1)}, bf16[8,3,12,1024]{3,0,2,1:T(8,128)(2,1)S(1)}, u32[]{:S(2)}, u32[]{:S(2)}) collective-permute-start(bf16[8,3,12,1024]{3,0,2,1:T(8,128)(2,1)S(1)} %copy.66), channel_id=1, source_target_pairs={{0,8},{8,16},{16,24},{1,9},{9,17},{17,25},{2,10},{10,18},{18,26},{... | collective-permute-start | bytes 1769480 | tf_op jit(solution)/shard_map/while/body/eval_jaxpr/ppermute | solution.py:12
  99.0 12.8 %collective-permute-start = (bf16[8,3,12,1024]{3,0,2,1:T(8,128)(2,1)S(1)}, bf16[8,3,12,1024]{3,0,2,1:T(8,128)(2,1)S(1)}, u32[]{:S(2)}, u32[]{:S(2)}) collective-permute-start(bf16[8,3,12,1024]{3,0,2,1:T(8,128)(2,1)S(1)} %copy.66), channel_id=1, source_target_pairs={{0,8},{8,16},{16,24},{1,9},{9,17},{17,25},{2,10},{10,18},{18,26},{... | collective-permute-start | bytes 1769480 | tf_op jit(solution)/shard_map/while/body/eval_jaxpr/ppermute | solution.py:12
  118.9 11.9 %collective-permute-start = (bf16[8,3,12,1024]{3,0,2,1:T(8,128)(2,1)S(1)}, bf16[8,3,12,1024]{3,0,2,1:T(8,128)(2,1)S(1)}, u32[]{:S(2)}, u32[]{:S(2)}) collective-permute-start(bf16[8,3,12,1024]{3,0,2,1:T(8,128)(2,1)S(1)} %copy.66), channel_id=1, source_target_pairs={{0,8},{8,16},{16,24},{1,9},{9,17},{17,25},{2,10},{10,18},{18,26},{... | collective-permute-start | bytes 1769480 | tf_op jit(solution)/shard_map/while/body/eval_jaxpr/ppermute | solution.py:12
  133.2 16.8 %collective-permute-start = (bf16[8,3,12,1024]{3,0,2,1:T(8,128)(2,1)S(1)}, bf16[8,3,12,1024]{3,0,2,1:T(8,128)(2,1)S(1)}, u32[]{:S(2)}, u32[]{:S(2)}) collective-permute-start(bf16[8,3,12,1024]{3,0,2,1:T(8,128)(2,1)S(1)} %copy.66), channel_id=1, source_target_pairs={{0,8},{8,16},{16,24},{1,9},{9,17},{17,25},{2,10},{10,18},{18,26},{... | collective-permute-start | bytes 1769480 | tf_op jit(solution)/shard_map/while/body/eval_jaxpr/ppermute | solution.py:12
  152.4 11.8 %collective-permute-start = (bf16[8,3,12,1024]{3,0,2,1:T(8,128)(2,1)S(1)}, bf16[8,3,12,1024]{3,0,2,1:T(8,128)(2,1)S(1)}, u32[]{:S(2)}, u32[]{:S(2)}) collective-permute-start(bf16[8,3,12,1024]{3,0,2,1:T(8,128)(2,1)S(1)} %copy.66), channel_id=1, source_target_pairs={{0,8},{8,16},{16,24},{1,9},{9,17},{17,25},{2,10},{10,18},{18,26},{... | collective-permute-start | bytes 1769480 | tf_op jit(solution)/shard_map/while/body/eval_jaxpr/ppermute | solution.py:12
  166.6 15.7 %collective-permute-start = (bf16[8,3,12,1024]{3,0,2,1:T(8,128)(2,1)S(1)}, bf16[8,3,12,1024]{3,0,2,1:T(8,128)(2,1)S(1)}, u32[]{:S(2)}, u32[]{:S(2)}) collective-permute-start(bf16[8,3,12,1024]{3,0,2,1:T(8,128)(2,1)S(1)} %copy.66), channel_id=1, source_target_pairs={{0,8},{8,16},{16,24},{1,9},{9,17},{17,25},{2,10},{10,18},{18,26},{... | collective-permute-start | bytes 1769480 | tf_op jit(solution)/shard_map/while/body/eval_jaxpr/ppermute | solution.py:12
Sparse Core Ops, SparseCore 0:
  235.4 32.9 reduce-scatter.1
where the time goes:
time: 276 us; the launch traced here: 275 us
  waiting for transfers between devices  109 us (39%)
  blocking collectives  46.8 us (17%)
  starting transfers between devices  41.9 us (15%)
  local copies, waits for them, and re-layouts  31.1 us (11%)
  matrix products  22 us (8%)
  between operations  13.5 us (5%)
  other arithmetic  10.4 us (4%)
    all_to_all x1, blocking collectives, on_device(): lax.all_to_all(slot_results.reshape(batches, rep_count, slot_count * capa...  46.8 us
    ppermute x7, waiting for transfers between devices, shifted(): return lax.ppermute(x, axis, pairs)  46.8 us
    ppermute x7, starting transfers between devices, shifted(): return lax.ppermute(x, axis, pairs)  36.5 us
    reduce_scatter x1, waiting for transfers between devices, on_device(): lax.psum_scatter(contribution.astype(jnp.bfloat16), 'section', scatter_di...  33.2 us
    all_to_all x1, waiting for transfers between devices, on_device(): lax.all_to_all(outgoing, 'rep', split_axis=1, concat_axis=1, tiled=True)  29.1 us
    select_n x14, local copies, waits for them, and re-layouts, tick(): outbuf = jnp.where(storing, stored, outbuf)  17.3 us
    dot_general x4, matrix products, update(): jnp.einsum('nscd,sde->nsce', lowered, section_weight, preferred_element_t...  17.3 us
  transfers between devices with their start and end apart: 9, of which 9 were waited for; matrix products, arithmetic and copies ran while one was open for 4% of the time, Pallas kernels for 0%

commit v1 on v0

--- a/solution.py
+++ b/solution.py
@@ -94,12 +94,20 @@
     start_slots = jnp.zeros((rep_count, slot_count, capacity, width_max), jnp.bfloat16)
     start_out = jnp.zeros((batches, rep_count, slot_count, capacity, width_max), jnp.bfloat16)
     last_slots, slot_results = lax.fori_loop(0, tick_count, tick, (start_slots, start_out))
-    returned = lax.all_to_all(
-        slot_results.reshape(batches, rep_count, slot_count * capacity, width_max),
-        "rep",
-        split_axis=1,
-        concat_axis=1,
-        tiled=True,
+    returned = jnp.concatenate(
+        lax.all_to_all(
+            jnp.stack(
+                jnp.split(
+                    slot_results.reshape(batches, rep_count, slot_count * capacity, width_max),
+                    lax.axis_size("rep"),
+                    axis=1,
+                )
+            ),
+            "rep",
+            0,
+            0,
+        ),
+        axis=1,
     )
     flat_back = returned.reshape(batches, total_slots * capacity, width_max)
     final_rows = jnp.einsum(

time: 276 us -> 290 us (1.051)
  local copies, waits for them, and re-layouts: 31.1 us -> 44.9 us
    split x0 -> x1, local copies, waits for them, and re-layouts: none -> 14.2 us  [on_device(): jnp.split(slot_results.reshape(batches, rep_count, slot_count * capacity,...]
    reshape x1 -> x0, local copies, waits for them, and re-layouts: 3.49 us -> none  [on_device(): slot_results.reshape(batches, rep_count, slot_count * capacity, width_max)]
where the time goes in v1:
time: 290 us; the launch traced here: 289 us
  waiting for transfers between devices  109 us (38%)
  blocking collectives  46.8 us (16%)
  local copies, waits for them, and re-layouts  44.9 us (15%)
  starting transfers between devices  42.1 us (15%)
  matrix products  22.1 us (8%)
  between operations  13.5 us (5%)
  other arithmetic  10.4 us (4%)
    ppermute x7, waiting for transfers between devices, shifted(): return lax.ppermute(x, axis, pairs)  46.9 us
    all_to_all x1, blocking collectives, on_device(): lax.all_to_all(jnp.stack(jnp.split(slot_results.reshape(batches, rep_coun...  46.8 us
    ppermute x7, starting transfers between devices, shifted(): return lax.ppermute(x, axis, pairs)  36.6 us
    reduce_scatter x1, waiting for transfers between devices, on_device(): lax.psum_scatter(contribution.astype(jnp.bfloat16), 'section', scatter_di...  33.1 us
    all_to_all x1, waiting for transfers between devices, on_device(): lax.all_to_all(outgoing, 'rep', split_axis=1, concat_axis=1, tiled=True)  28.9 us
    dot_general x4, matrix products, update(): jnp.einsum('nscd,sde->nsce', lowered, section_weight, preferred_element_t...  17.4 us
    select_n x14, local copies, waits for them, and re-layouts, tick(): outbuf = jnp.where(storing, stored, outbuf)  17.3 us
    split x1, local copies, waits for them, and re-layouts, on_device(): jnp.split(slot_results.reshape(batches, rep_count, slot_count * capacity,...  14.2 us
  transfers between devices with their start and end apart: 9, of which 9 were waited for; matrix products, arithmetic and copies ran while one was open for 4% of the time, Pallas kernels for 0%

profile of v1, /device:TPU:0, one launch (start us, length us, event | category | flops | bytes accessed | tf_op | source)
XLA Modules:
  0.0 289.3 jit_solution(1530068219935787646)
XLA Ops:
  8.0 2.1 convolution_convert_fusion
  10.1 3.2 %copy.188 = bf16[4,288,1024]{2,0,1:T(4,128)(2,1)} copy(bf16[4,288,1024]{2,1,0:T(8,128)(2,1)S(1)} %convolution_convert_fusion) | data formatting | bytes 4718592 | tf_op jit(solution)/shard_map/convert_element_type | solution.py:75
  13.4 5.3 %all-to-all-start = ((bf16[4,8,36,1024]{3,0,2,1:T(4,128)(2,1)}), bf16[4,8,36,1024]{3,0,2,1:T(4,128)(2,1)S(1)}, u32[]{:S(2)}, u32[]{:S(2)}) async-start(bf16[4,8,36,1024]{3,0,2,1:T(4,128)(2,1)} %bitcast.55), calls=%async_computation | async-start | bytes 4718592 | tf_op jit(solution)/shard_map/all_to_all | solution.py:77
  19.2 28.9 %all-to-all-done = bf16[4,8,36,1024]{3,0,2,1:T(4,128)(2,1)S(1)} async-done(((bf16[4,8,36,1024]{3,0,2,1:T(4,128)(2,1)}), bf16[4,8,36,1024]{3,0,2,1:T(4,128)(2,1)S(1)}, u32[]{:S(2)}, u32[]{:S(2)}) %all-to-all-start) | async-done | bytes 2359328 | tf_op jit(solution)/shard_map/all_to_all | solution.py:77
  48.1 2.7 copy.189
  50.9 1.7 broadcast_in_dim.47.clone
  52.6 129.9 %while.17 = (s32[]{:T(128)}, bf16[8,3,12,1024]{3,0,2,1:T(8,128)(2,1)S(1)}, bf16[4,8,3,12,1024]{4,1,3,2,0:T(8,128)(2,1)}, s32[]{:T(128)}, pred[]{:T(512)}, /*inde...) while((s32[]{:T(128)}, ...), condition=%wide.region_9.10_spmd.clone, body=%wide.region_5.9_spmd.clone.sunk | while | flops 608999680 | bytes 19899208 | solution.py:96
  54.6 4.7 %conditional.3 = (bf16[8,3,12,1024]{3,2,0,1:T(8,128)(2,1)S(1)}) conditional(s32[]{:T(128)} %convert_element_type.86, bf16[8,3,12,1024]{3,2,0,1:T(8,128)(2,1)S(1)} %bitcast_select_fusion.2, (bf16[8,3,12,1024]{3,2,0,1:T(8,128)(2,1)S(1)}, f32[3]{0:T(128)S(1)}, f32[1,3,1024]{2,1,0:T(4,128)S(1)}, bf16[3,1024,1024]{2,1,0:T(8,128)(2,1)}, ...), branch_computations={%region_6.6_spmd, %region_7.8_spmd} | conditional | flops 608403712 | bytes 9269780 | solution.py:87
  55.0 4.3 %fusion.7 = bf16[8,3,12,1024]{3,2,0,1:T(8,128)(2,1)S(1)} fusion(bf16[8,3,12,1024]{3,2,0,1:T(8,128)(2,1)S(1)} %copy.253, bf16[3,1024,1024]{2,1,0:T(8,128)(2,1)} %get-tuple-element.218, f32[3,1024]{1,0:T(4,128)S(1)} %get-tuple-element.219, f32[3,1024]{1,0:T(4,128)S(1)} %bitcast.57, f32[8,3,12]{2,0,1:T(8,128)S(1)} %add_rsqrt_fusion), kind=kOutput, calls=%fused_computation.9 | convolution fusion | flops 607518720 | bytes 7496832 | tf_op jit(solution)/shard_map/while/body/eval_jaxpr/cond/branch_1_fun/nscd,sde->nsce/dot_general | solution.py:58
  62.6 8.6 %collective-permute-done = bf16[8,3,12,1024]{3,0,2,1:T(8,128)(2,1)S(1)} collective-permute-done((bf16[8,3,12,1024]{3,0,2,1:T(8,128)(2,1)S(1)}, bf16[8,3,12,1024]{3,0,2,1:T(8,128)(2,1)S(1)}, u32[]{:S(2)}, u32[]{:S(2)}) %collective-permute-start) | collective-permute-done | bytes 589856 | tf_op jit(solution)/shard_map/while/body/eval_jaxpr/ppermute | solution.py:12
  73.2 4.8 %conditional.3 = (bf16[8,3,12,1024]{3,2,0,1:T(8,128)(2,1)S(1)}) conditional(s32[]{:T(128)} %convert_element_type.86, bf16[8,3,12,1024]{3,2,0,1:T(8,128)(2,1)S(1)} %bitcast_select_fusion.2, (bf16[8,3,12,1024]{3,2,0,1:T(8,128)(2,1)S(1)}, f32[3]{0:T(128)S(1)}, f32[1,3,1024]{2,1,0:T(4,128)S(1)}, bf16[3,1024,1024]{2,1,0:T(8,128)(2,1)}, ...), branch_computations={%region_6.6_spmd, %region_7.8_spmd} | conditional | flops 608403712 | bytes 9269780 | solution.py:87
  73.6 4.4 %fusion.7 = bf16[8,3,12,1024]{3,2,0,1:T(8,128)(2,1)S(1)} fusion(bf16[8,3,12,1024]{3,2,0,1:T(8,128)(2,1)S(1)} %copy.253, bf16[3,1024,1024]{2,1,0:T(8,128)(2,1)} %get-tuple-element.218, f32[3,1024]{1,0:T(4,128)S(1)} %get-tuple-element.219, f32[3,1024]{1,0:T(4,128)S(1)} %bitcast.57, f32[8,3,12]{2,0,1:T(8,128)S(1)} %add_rsqrt_fusion), kind=kOutput, calls=%fused_computation.9 | convolution fusion | flops 607518720 | bytes 7496832 | tf_op jit(solution)/shard_map/while/body/eval_jaxpr/cond/branch_1_fun/nscd,sde->nsce/dot_general | solution.py:58
  78.3 4.4 %collective-permute-start = (bf16[8,3,12,1024]{3,0,2,1:T(8,128)(2,1)S(1)}, bf16[8,3,12,1024]{3,0,2,1:T(8,128)(2,1)S(1)}, u32[]{:S(2)}, u32[]{:S(2)}) collective-permute-start(bf16[8,3,12,1024]{3,0,2,1:T(8,128)(2,1)S(1)} %copy.232), channel_id=1, source_target_pairs={{0,8},{8,16},{16,24},{1,9},{9,17},{17,25},{2,10},{10,18},{18,26},{... | collective-permute-start | bytes 1769480 | tf_op jit(solution)/shard_map/while/body/eval_jaxpr/ppermute | solution.py:12
  84.2 7.7 %collective-permute-done = bf16[8,3,12,1024]{3,0,2,1:T(8,128)(2,1)S(1)} collective-permute-done((bf16[8,3,12,1024]{3,0,2,1:T(8,128)(2,1)S(1)}, bf16[8,3,12,1024]{3,0,2,1:T(8,128)(2,1)S(1)}, u32[]{:S(2)}, u32[]{:S(2)}) %collective-permute-start) | collective-permute-done | bytes 589856 | tf_op jit(solution)/shard_map/while/body/eval_jaxpr/ppermute | solution.py:12
  94.0 4.8 %conditional.3 = (bf16[8,3,12,1024]{3,2,0,1:T(8,128)(2,1)S(1)}) conditional(s32[]{:T(128)} %convert_element_type.86, bf16[8,3,12,1024]{3,2,0,1:T(8,128)(2,1)S(1)} %bitcast_select_fusion.2, (bf16[8,3,12,1024]{3,2,0,1:T(8,128)(2,1)S(1)}, f32[3]{0:T(128)S(1)}, f32[1,3,1024]{2,1,0:T(4,128)S(1)}, bf16[3,1024,1024]{2,1,0:T(8,128)(2,1)}, ...), branch_computations={%region_6.6_spmd, %region_7.8_spmd} | conditional | flops 608403712 | bytes 9269780 | solution.py:87
  94.4 4.4 %fusion.7 = bf16[8,3,12,1024]{3,2,0,1:T(8,128)(2,1)S(1)} fusion(bf16[8,3,12,1024]{3,2,0,1:T(8,128)(2,1)S(1)} %copy.253, bf16[3,1024,1024]{2,1,0:T(8,128)(2,1)} %get-tuple-element.218, f32[3,1024]{1,0:T(4,128)S(1)} %get-tuple-element.219, f32[3,1024]{1,0:T(4,128)S(1)} %bitcast.57, f32[8,3,12]{2,0,1:T(8,128)S(1)} %add_rsqrt_fusion), kind=kOutput, calls=%fused_computation.9 | convolution fusion | flops 607518720 | bytes 7496832 | tf_op jit(solution)/shard_map/while/body/eval_jaxpr/cond/branch_1_fun/nscd,sde->nsce/dot_general | solution.py:58
  99.1 4.4 %collective-permute-start = (bf16[8,3,12,1024]{3,0,2,1:T(8,128)(2,1)S(1)}, bf16[8,3,12,1024]{3,0,2,1:T(8,128)(2,1)S(1)}, u32[]{:S(2)}, u32[]{:S(2)}) collective-permute-start(bf16[8,3,12,1024]{3,0,2,1:T(8,128)(2,1)S(1)} %copy.232), channel_id=1, source_target_pairs={{0,8},{8,16},{16,24},{1,9},{9,17},{17,25},{2,10},{10,18},{18,26},{... | collective-permute-start | bytes 1769480 | tf_op jit(solution)/shard_map/while/body/eval_jaxpr/ppermute | solution.py:12
  105.0 6.9 %collective-permute-done = bf16[8,3,12,1024]{3,0,2,1:T(8,128)(2,1)S(1)} collective-permute-done((bf16[8,3,12,1024]{3,0,2,1:T(8,128)(2,1)S(1)}, bf16[8,3,12,1024]{3,0,2,1:T(8,128)(2,1)S(1)}, u32[]{:S(2)}, u32[]{:S(2)}) %collective-permute-start) | collective-permute-done | bytes 589856 | tf_op jit(solution)/shard_map/while/body/eval_jaxpr/ppermute | solution.py:12
  113.9 4.8 %conditional.3 = (bf16[8,3,12,1024]{3,2,0,1:T(8,128)(2,1)S(1)}) conditional(s32[]{:T(128)} %convert_element_type.86, bf16[8,3,12,1024]{3,2,0,1:T(8,128)(2,1)S(1)} %bitcast_select_fusion.2, (bf16[8,3,12,1024]{3,2,0,1:T(8,128)(2,1)S(1)}, f32[3]{0:T(128)S(1)}, f32[1,3,1024]{2,1,0:T(4,128)S(1)}, bf16[3,1024,1024]{2,1,0:T(8,128)(2,1)}, ...), branch_computations={%region_6.6_spmd, %region_7.8_spmd} | conditional | flops 608403712 | bytes 9269780 | solution.py:87
  114.3 4.4 %fusion.7 = bf16[8,3,12,1024]{3,2,0,1:T(8,128)(2,1)S(1)} fusion(bf16[8,3,12,1024]{3,2,0,1:T(8,128)(2,1)S(1)} %copy.253, bf16[3,1024,1024]{2,1,0:T(8,128)(2,1)} %get-tuple-element.218, f32[3,1024]{1,0:T(4,128)S(1)} %get-tuple-element.219, f32[3,1024]{1,0:T(4,128)S(1)} %bitcast.57, f32[8,3,12]{2,0,1:T(8,128)S(1)} %add_rsqrt_fusion), kind=kOutput, calls=%fused_computation.9 | convolution fusion | flops 607518720 | bytes 7496832 | tf_op jit(solution)/shard_map/while/body/eval_jaxpr/cond/branch_1_fun/nscd,sde->nsce/dot_general | solution.py:58
  119.0 4.4 %collective-permute-start = (bf16[8,3,12,1024]{3,0,2,1:T(8,128)(2,1)S(1)}, bf16[8,3,12,1024]{3,0,2,1:T(8,128)(2,1)S(1)}, u32[]{:S(2)}, u32[]{:S(2)}) collective-permute-start(bf16[8,3,12,1024]{3,0,2,1:T(8,128)(2,1)S(1)} %copy.232), channel_id=1, source_target_pairs={{0,8},{8,16},{16,24},{1,9},{9,17},{17,25},{2,10},{10,18},{18,26},{... | collective-permute-start | bytes 1769480 | tf_op jit(solution)/shard_map/while/body/eval_jaxpr/ppermute | solution.py:12
  125.0 6.0 %collective-permute-done = bf16[8,3,12,1024]{3,0,2,1:T(8,128)(2,1)S(1)} collective-permute-done((bf16[8,3,12,1024]{3,0,2,1:T(8,128)(2,1)S(1)}, bf16[8,3,12,1024]{3,0,2,1:T(8,128)(2,1)S(1)}, u32[]{:S(2)}, u32[]{:S(2)}) %collective-permute-start) | collective-permute-done | bytes 589856 | tf_op jit(solution)/shard_map/while/body/eval_jaxpr/ppermute | solution.py:12
  133.4 9.2 %collective-permute-start = (bf16[8,3,12,1024]{3,0,2,1:T(8,128)(2,1)S(1)}, bf16[8,3,12,1024]{3,0,2,1:T(8,128)(2,1)S(1)}, u32[]{:S(2)}, u32[]{:S(2)}) collective-permute-start(bf16[8,3,12,1024]{3,0,2,1:T(8,128)(2,1)S(1)} %copy.232), channel_id=1, source_target_pairs={{0,8},{8,16},{16,24},{1,9},{9,17},{17,25},{2,10},{10,18},{18,26},{... | collective-permute-start | bytes 1769480 | tf_op jit(solution)/shard_map/while/body/eval_jaxpr/ppermute | solution.py:12
  144.0 6.1 %collective-permute-done = bf16[8,3,12,1024]{3,0,2,1:T(8,128)(2,1)S(1)} collective-permute-done((bf16[8,3,12,1024]{3,0,2,1:T(8,128)(2,1)S(1)}, bf16[8,3,12,1024]{3,0,2,1:T(8,128)(2,1)S(1)}, u32[]{:S(2)}, u32[]{:S(2)}) %collective-permute-start) | collective-permute-done | bytes 589856 | tf_op jit(solution)/shard_map/while/body/eval_jaxpr/ppermute | solution.py:12
  152.6 4.4 %collective-permute-start = (bf16[8,3,12,1024]{3,0,2,1:T(8,128)(2,1)S(1)}, bf16[8,3,12,1024]{3,0,2,1:T(8,128)(2,1)S(1)}, u32[]{:S(2)}, u32[]{:S(2)}) collective-permute-start(bf16[8,3,12,1024]{3,0,2,1:T(8,128)(2,1)S(1)} %copy.232), channel_id=1, source_target_pairs={{0,8},{8,16},{16,24},{1,9},{9,17},{17,25},{2,10},{10,18},{18,26},{... | collective-permute-start | bytes 1769480 | tf_op jit(solution)/shard_map/while/body/eval_jaxpr/ppermute | solution.py:12
  158.5 5.8 %collective-permute-done = bf16[8,3,12,1024]{3,0,2,1:T(8,128)(2,1)S(1)} collective-permute-done((bf16[8,3,12,1024]{3,0,2,1:T(8,128)(2,1)S(1)}, bf16[8,3,12,1024]{3,0,2,1:T(8,128)(2,1)S(1)}, u32[]{:S(2)}, u32[]{:S(2)}) %collective-permute-start) | collective-permute-done | bytes 589856 | tf_op jit(solution)/shard_map/while/body/eval_jaxpr/ppermute | solution.py:12
  166.7 8.4 %collective-permute-start = (bf16[8,3,12,1024]{3,0,2,1:T(8,128)(2,1)S(1)}, bf16[8,3,12,1024]{3,0,2,1:T(8,128)(2,1)S(1)}, u32[]{:S(2)}, u32[]{:S(2)}) collective-permute-start(bf16[8,3,12,1024]{3,0,2,1:T(8,128)(2,1)S(1)} %copy.232), channel_id=1, source_target_pairs={{0,8},{8,16},{16,24},{1,9},{9,17},{17,25},{2,10},{10,18},{18,26},{... | collective-permute-start | bytes 1769480 | tf_op jit(solution)/shard_map/while/body/eval_jaxpr/ppermute | solution.py:12
  176.7 5.8 %collective-permute-done = bf16[8,3,12,1024]{3,0,2,1:T(8,128)(2,1)S(1)} collective-permute-done((bf16[8,3,12,1024]{3,0,2,1:T(8,128)(2,1)S(1)}, bf16[8,3,12,1024]{3,0,2,1:T(8,128)(2,1)S(1)}, u32[]{:S(2)}, u32[]{:S(2)}) %collective-permute-start) | collective-permute-done | bytes 589856 | tf_op jit(solution)/shard_map/while/body/eval_jaxpr/ppermute | solution.py:12
  182.5 14.2 %fusion.35 = (bf16[4,1,36,1024]{3,1,2,0:T(2,128)(2,1)S(1)}, bf16[4,1,36,1024]{3,1,2,0:T(2,128)(2,1)S(1)}, bf16[4,1,36,1024]{3,1,2,0:T(2,128)(2,1)S(1)}, bf16[4,1...) fusion(bf16[4,8,36,1024]{3,1,2,0:T(8,128)(2,1)} %bitcast.8), kind=kLoop, calls=%fused_computation.57 | loop fusion | bytes 4718592 | tf_op jit(solution)/shard_map/split | solution.py:100
  199.9 46.8 %all_to_all.10 = bf16[8,4,1,36,1024]{4,1,3,2,0:T(4,128)(2,1)S(1)} all-to-all(bf16[8,4,1,36,1024]{4,1,3,2,0:T(4,128)(2,1)S(1)} %bitcast_dynamic-update-slice_fusion), channel_id=1, replica_groups=mesh['section'=4,'rep'=8] {'rep'}, dimensions={0} | all-to-all | bytes 4718592 | tf_op jit(solution)/shard_map/all_to_all | solution.py:98
  246.8 2.6 select_convert_fusion
  249.4 33.1 %reduce-scatter.2.cloned.1.call-done = bf16[4,128,256]{2,1,0:T(8,128)(2,1)} async-done(((bf16[4,128,1024]{2,1,0:T(8,128)(2,1)}), bf16[4,128,256]{2,1,0:T(8,128)(2,1)}) %reduce-scatter.2.cloned.1.call-update) | async-done | bytes 262160 | tf_op jit(solution)/shard_map/reduce_scatter | solution.py:119
  (84 shorter events, 35.1 us)
Async XLA Ops:
  13.3 5.6 %copy-start = (f32[1,3,1024]{2,0,1:T(1,128)S(1)}, f32[1,3,1024]{2,0,1:T(1,128)}, u32[]{:S(2)}) copy-start(f32[1,3,1024]{2,0,1:T(1,128)} %param.14) | copy-start | bytes 36868
  13.3 5.6 %copy-start.1 = (s32[16]{0:T(128)S(1)}, s32[16]{0:T(128)}, u32[]{:S(2)}) copy-start(s32[16]{0:T(128)} %param.13) | copy-start | bytes 196
  13.3 5.6 %copy-start.2 = (s32[16]{0:T(128)S(1)}, s32[16]{0:T(128)}, u32[]{:S(2)}) copy-start(s32[16]{0:T(128)} %param.12) | copy-start | bytes 196
  13.4 34.8 %all-to-all-start = ((bf16[4,8,36,1024]{3,0,2,1:T(4,128)(2,1)}), bf16[4,8,36,1024]{3,0,2,1:T(4,128)(2,1)S(1)}, u32[]{:S(2)}, u32[]{:S(2)}) async-start(bf16[4,8,36,1024]{3,0,2,1:T(4,128)(2,1)} %bitcast.55), calls=%async_computation | async-start | bytes 4718592 | tf_op jit(solution)/shard_map/all_to_all | solution.py:77
  18.7 263.8 %reduce-scatter.2.cloned.1.call-start = ((), (), s32[]{:S(2)}) async-start(), calls=%async_computation.3 | async-start | bytes 1310720 | tf_op jit(solution)/shard_map/reduce_scatter | solution.py:119
  59.7 11.4 %collective-permute-start = (bf16[8,3,12,1024]{3,0,2,1:T(8,128)(2,1)S(1)}, bf16[8,3,12,1024]{3,0,2,1:T(8,128)(2,1)S(1)}, u32[]{:S(2)}, u32[]{:S(2)}) collective-permute-start(bf16[8,3,12,1024]{3,0,2,1:T(8,128)(2,1)S(1)} %copy.232), channel_id=1, source_target_pairs={{0,8},{8,16},{16,24},{1,9},{9,17},{17,25},{2,10},{10,18},{18,26},{... | collective-permute-start | bytes 1769480 | tf_op jit(solution)/shard_map/while/body/eval_jaxpr/ppermute | solution.py:12
  78.3 13.6 %collective-permute-start = (bf16[8,3,12,1024]{3,0,2,1:T(8,128)(2,1)S(1)}, bf16[8,3,12,1024]{3,0,2,1:T(8,128)(2,1)S(1)}, u32[]{:S(2)}, u32[]{:S(2)}) collective-permute-start(bf16[8,3,12,1024]{3,0,2,1:T(8,128)(2,1)S(1)} %copy.232), channel_id=1, source_target_pairs={{0,8},{8,16},{16,24},{1,9},{9,17},{17,25},{2,10},{10,18},{18,26},{... | collective-permute-start | bytes 1769480 | tf_op jit(solution)/shard_map/while/body/eval_jaxpr/ppermute | solution.py:12
  99.1 12.8 %collective-permute-start = (bf16[8,3,12,1024]{3,0,2,1:T(8,128)(2,1)S(1)}, bf16[8,3,12,1024]{3,0,2,1:T(8,128)(2,1)S(1)}, u32[]{:S(2)}, u32[]{:S(2)}) collective-permute-start(bf16[8,3,12,1024]{3,0,2,1:T(8,128)(2,1)S(1)} %copy.232), channel_id=1, source_target_pairs={{0,8},{8,16},{16,24},{1,9},{9,17},{17,25},{2,10},{10,18},{18,26},{... | collective-permute-start | bytes 1769480 | tf_op jit(solution)/shard_map/while/body/eval_jaxpr/ppermute | solution.py:12
  119.0 11.9 %collective-permute-start = (bf16[8,3,12,1024]{3,0,2,1:T(8,128)(2,1)S(1)}, bf16[8,3,12,1024]{3,0,2,1:T(8,128)(2,1)S(1)}, u32[]{:S(2)}, u32[]{:S(2)}) collective-permute-start(bf16[8,3,12,1024]{3,0,2,1:T(8,128)(2,1)S(1)} %copy.232), channel_id=1, source_target_pairs={{0,8},{8,16},{16,24},{1,9},{9,17},{17,25},{2,10},{10,18},{18,26},{... | collective-permute-start | bytes 1769480 | tf_op jit(solution)/shard_map/while/body/eval_jaxpr/ppermute | solution.py:12
  133.4 16.8 %collective-permute-start = (bf16[8,3,12,1024]{3,0,2,1:T(8,128)(2,1)S(1)}, bf16[8,3,12,1024]{3,0,2,1:T(8,128)(2,1)S(1)}, u32[]{:S(2)}, u32[]{:S(2)}) collective-permute-start(bf16[8,3,12,1024]{3,0,2,1:T(8,128)(2,1)S(1)} %copy.232), channel_id=1, source_target_pairs={{0,8},{8,16},{16,24},{1,9},{9,17},{17,25},{2,10},{10,18},{18,26},{... | collective-permute-start | bytes 1769480 | tf_op jit(solution)/shard_map/while/body/eval_jaxpr/ppermute | solution.py:12
  152.6 11.8 %collective-permute-start = (bf16[8,3,12,1024]{3,0,2,1:T(8,128)(2,1)S(1)}, bf16[8,3,12,1024]{3,0,2,1:T(8,128)(2,1)S(1)}, u32[]{:S(2)}, u32[]{:S(2)}) collective-permute-start(bf16[8,3,12,1024]{3,0,2,1:T(8,128)(2,1)S(1)} %copy.232), channel_id=1, source_target_pairs={{0,8},{8,16},{16,24},{1,9},{9,17},{17,25},{2,10},{10,18},{18,26},{... | collective-permute-start | bytes 1769480 | tf_op jit(solution)/shard_map/while/body/eval_jaxpr/ppermute | solution.py:12
  166.7 15.8 %collective-permute-start = (bf16[8,3,12,1024]{3,0,2,1:T(8,128)(2,1)S(1)}, bf16[8,3,12,1024]{3,0,2,1:T(8,128)(2,1)S(1)}, u32[]{:S(2)}, u32[]{:S(2)}) collective-permute-start(bf16[8,3,12,1024]{3,0,2,1:T(8,128)(2,1)S(1)} %copy.232), channel_id=1, source_target_pairs={{0,8},{8,16},{16,24},{1,9},{9,17},{17,25},{2,10},{10,18},{18,26},{... | collective-permute-start | bytes 1769480 | tf_op jit(solution)/shard_map/while/body/eval_jaxpr/ppermute | solution.py:12
Sparse Core Ops, SparseCore 0:
  249.5 32.9 reduce-scatter.1
